TPU v7x, 32 devices: a whole 2x2x4 slice. The times are simulated.
32 devices in a mesh: row: 8 (over z, core), col: 4 (over y, x).
Axes of the slice: x: 2, y: 2, z: 4, core: 2. Of those that a mesh axis runs over, the one named last changes fastest.
Arguments:
- grm_prior: float32 [1024, 1024], P('row', 'col'), may hold values from -0.6 to 0.6
- dosage_now: bfloat16 [1024, 4096], P('row', 'col'), may hold values from 0 to 2
- mask_now: int32 [1024, 4096], P('row', 'col'), may hold values 0 or 1
- dosage_prev: bfloat16 [1024, 256], P('row'), may hold values from 0 to 2
- mask_prev: int32 [1024, 256], P('row'), may hold values 0 or 1
- expression: bfloat16 [1024, 20480], P('row', 'col'), may hold values from -18 to 18
Outputs:
- grm_total: float32 [1024, 1024], P('row', 'col')
- assoc_score: float32 [256, 20480], P('row', 'col')
All inputs are finite; a program needn't handle non-finite values. No bound on the sum of `mask_now` or of `mask_prev` on one device may be relied on, other than what follows from the above.
Results may differ from a plain program's by a relative error of at most 0.0029.
Values may be sent and summed in bfloat16 or wider, within the bound.
A program may use at most 64 MiB of HBM per device.

v0:
```python
import math

import jax
import jax.numpy as jnp
from jax import lax
from jax.sharding import PartitionSpec as P

VARIANTS = 4096


epsilon = 1e-05


def spread(value, axis, source):
    kept = jnp.where(lax.axis_index(axis) == source, value, 0).astype(value.dtype)
    return lax.psum(kept, axis)


def local_sums(dosage, present):
    values = dosage.astype(jnp.float32)
    weight = present.astype(jnp.float32)
    return (values, weight, jnp.sum(weight, 0), jnp.sum(weight * values, 0))


def body(grm_prior, dosage_now, mask_now, dosage_prev, mask_prev, expression):
    samples_all = dosage_now.shape[0] * lax.axis_size("row")
    values_now, weight_now, seen_now, summed_now = local_sums(dosage_now, mask_now)
    values_prev, weight_prev, seen_prev, summed_prev = local_sums(dosage_prev, mask_prev)
    traits = expression.astype(jnp.float32)
    squares_trait = jnp.sum(traits * traits, 0)
    seen_now, summed_now, seen_prev, summed_prev, squares_trait = lax.psum(
        (seen_now, summed_now, seen_prev, summed_prev, squares_trait), "row"
    )
    observed_now = jnp.maximum(seen_now, 1.0)
    observed_prev = jnp.maximum(seen_prev, 1.0)
    offset_now = weight_now * (values_now - summed_now / observed_now)
    offset_prev = weight_prev * (values_prev - summed_prev / observed_prev)
    second_now, second_prev = lax.psum(
        (jnp.sum(offset_now * offset_now, 0), jnp.sum(offset_prev * offset_prev, 0)), "row"
    )
    spread_now = second_now / observed_now
    spread_prev = second_prev / observed_prev
    scaled = (offset_now * lax.rsqrt(spread_now + epsilon)).astype(jnp.bfloat16)
    own_panel = lax.all_gather(scaled, "col", axis=1, tiled=True)
    panels = lax.axis_size("row") // lax.axis_size("col")
    column = lax.axis_index("col")
    blocks = []
    for member in range(panels):
        remote = spread(own_panel, "row", column * panels + member)
        blocks.append(
            lax.dot_general(
                own_panel, remote, (((1,), (1,)), ((), ())), preferred_element_type=jnp.float32
            )
        )
    grm_total = grm_prior + jnp.concatenate(blocks, 1) / VARIANTS
    genotype = offset_prev.astype(jnp.bfloat16)
    out_rows = genotype.shape[1] // lax.axis_size("row")
    first_row = lax.axis_index("row") * out_rows
    cross_sum = lax.psum_scatter(
        lax.dot_general(
            genotype, expression, (((0,), (0,)), ((), ())), preferred_element_type=jnp.float32
        ),
        "row",
        scatter_dimension=0,
        tiled=True,
    )
    spread_rows = lax.dynamic_slice_in_dim(spread_prev, first_row, out_rows, 0)
    power = squares_trait / samples_all
    assoc_score = (
        cross_sum
        * lax.rsqrt(spread_rows + epsilon)[:, None]
        * lax.rsqrt(power + epsilon)[None, :]
        / math.sqrt(samples_all)
    )
    return (grm_total, assoc_score)


def solution(mesh):
    in_specs = (
        P("row", "col"),
        P("row", "col"),
        P("row", "col"),
        P("row", None),
        P("row", None),
        P("row", "col"),
    )
    out_specs = (P("row", "col"), P("row", "col"))
    return jax.shard_map(body, mesh=mesh, in_specs=in_specs, out_specs=out_specs, check_vma=False)
```

profile of v0, /device:TPU:0, one launch (start us, length us, event | category | flops | bytes accessed | tf_op | source)
XLA Modules:
  0.0 232.5 jit_solution(1334787050042367653)
XLA Ops:
  7.2 0.0 all-gather.2.cloned.1.call-start
  7.2 1.3 convert_reduce_fusion
  8.6 1.0 convert_reduce_fusion.1
  9.6 30.3 %all-reduce.1 = (f32[1024]{0:T(1024)S(1)}, f32[1024]{0:T(1024)S(1)}, f32[256]{0:T(256)S(1)}, f32[256]{0:T(256)S(1)}) all-reduce(f32[1024]{0:T(1024)S(1)} %get-tuple-element.5, f32[1024]{0:T(1024)S(1)} %get-tuple-element.4, f32[256]{0:T(256)S(1)} %get-tuple-element.7, ...), channel_id=1, replica_groups=mesh['row'=8,'col'=4] {'row'}, use_global_device_ids=true, to_apply=%region_1.0 | all-reduce | flops 2560 | bytes 20480 | tf_op jit(solution)/shard_map/psum | solution.py:31
  39.9 1.1 multiply_reduce_fusion.1
  41.0 0.9 multiply_reduce_fusion.2
  41.9 0.3 multiply_reduce_fusion
  42.2 26.0 %all-reduce = (f32[1024]{0:T(1024)S(1)}, f32[5120]{0:T(1024)S(1)}, f32[256]{0:T(256)S(1)}) all-reduce(f32[1024]{0:T(1024)S(1)} %multiply_reduce_fusion.1, f32[5120]{0:T(1024)S(1)} %multiply_reduce_fusion, f32[256]{0:T(256)S(1)} %multiply_reduce_fusion.2), channel_id=1, replica_groups=mesh['row'=8,'col'=4] {'row'}, use_global_device_ids=true, to_apply=%region_5.0 | all-reduce | flops 6400 | bytes 51200 | tf_op jit(solution)/shard_map/psum | solution.py:38
  68.2 0.8 multiply_convert_fusion
  69.0 0.0 all-reduce.5.cloned.1.call-start
  69.1 24.8 %all-gather.2.cloned.1.call-done = bf16[128,4096]{1,0:T(8,128)(2,1)} async-done(((bf16[128,1024]{1,0:T(8,128)(2,1)}), bf16[128,4096]{1,0:T(8,128)(2,1)}) %all-gather.2.cloned.1.call-update) | async-done | bytes 1048592 | tf_op jit(solution)/shard_map/all_gather | solution.py:44
  93.9 2.8 %broadcast_select_fusion.1 = (bf16[128,4096]{1,0:T(8,128)(2,1)}, bf16[128,4096]{1,0:T(8,128)(2,1)}) fusion(bf16[128,4096]{1,0:T(8,128)(2,1)} %all-gather.2.cloned.1.call-done, pred[]{:T(512)S(6)} %eq.6, pred[]{:T(512)S(6)} %eq.7), kind=kLoop, calls=%fused_computation.2 | loop fusion | flops 1048576 | bytes 3145730 | tf_op jit(solution)/shard_map/jit(_where)/select_n | solution.py:15
  96.7 0.0 reduce-scatter.2.cloned.1.call-start
  96.7 0.8 copy-done.6
  97.5 3.2 %fusion.6 = f32[256,5120]{1,0:T(8,128)} fusion(bf16[128,5120]{1,0:T(8,128)(2,1)S(1)} %copy-done.1, bf16[128,256]{1,0:T(8,128)(2,1)S(1)} %copy-done.6, s32[128,256]{1,0:T(8,128)S(1)} %copy-done.4, f32[256]{0:T(256)S(1)} %maximum_divide_fusion.2), kind=kOutput, calls=%fused_computation.20 | convolution fusion | flops 335708160 | bytes 6751232 | tf_op jit(solution)/shard_map/dot_general | solution.py:60
  100.7 0.9 copy-done.7
  101.6 0.1 copy.8
  101.7 0.1 add_rsqrt_fusion.2
  101.8 60.3 %all-reduce.5.cloned.1.call-done = (bf16[128,4096]{1,0:T(8,128)(2,1)}, bf16[128,4096]{1,0:T(8,128)(2,1)}) async-done(((bf16[128,4096]{1,0:T(8,128)(2,1)}, bf16[128,4096]{1,0:T(8,128)(2,1)}), (bf16[128,4096]{1,0:T(8,128)(2,1)}, bf16[128,4096]{1,0:T(8,128)(2,1)})) %all-reduce.5.cloned.1.call-update) | async-done | bytes 2097168 | tf_op jit(solution)/shard_map/psum | solution.py:16
  162.1 1.7 fusion.9
  163.8 0.5 fusion.10
  164.4 0.8 copy.9
  165.2 58.7 %reduce-scatter.2.cloned.1.call-done = f32[32,5120]{1,0:T(8,128)} async-done(((f32[256,5120]{1,0:T(8,128)}), f32[32,5120]{1,0:T(8,128)}) %reduce-scatter.2.cloned.1.call-update) | async-done | bytes 655376 | tf_op jit(solution)/shard_map/reduce_scatter | solution.py:59
  223.9 2.1 multiply_multiply_fusion
  (23 shorter events, 0.1 us)
Async XLA Ops:
  7.2 32.7 %copy-start.2 = (s32[128,1024]{1,0:T(8,128)S(1)}, s32[128,1024]{1,0:T(8,128)}, u32[]{:S(2)}) copy-start(s32[128,1024]{1,0:T(8,128)} %param.8) | copy-start | bytes 1572868
  7.2 33.8 %copy-start.4 = (s32[128,256]{1,0:T(8,128)S(1)}, s32[128,256]{1,0:T(8,128)}, u32[]{:S(2)}) copy-start(s32[128,256]{1,0:T(8,128)} %param.10) | copy-start | bytes 393220
  7.2 34.7 %copy-start.1 = (bf16[128,5120]{1,0:T(8,128)(2,1)S(1)}, bf16[128,5120]{1,0:T(8,128)(2,1)}, u32[]{:S(2)}) copy-start(bf16[128,5120]{1,0:T(8,128)(2,1)} %param.11) | copy-start | bytes 3932164
  7.2 86.7 %all-gather.2.cloned.1.call-start = ((), (), s32[]{:S(2)}) async-start(), calls=%async_computation.1 | async-start | bytes 1310720 | tf_op jit(solution)/shard_map/all_gather | solution.py:44
  8.6 59.6 %copy-start.3 = (bf16[128,1024]{1,0:T(8,128)(2,1)S(1)}, bf16[128,1024]{1,0:T(8,128)(2,1)}, u32[]{:S(2)}) copy-start(bf16[128,1024]{1,0:T(8,128)(2,1)} %param.7) | copy-start | bytes 786436
  69.0 93.1 %all-reduce.5.cloned.1.call-start = ((), (), s32[]{:S(2)}) async-start(), calls=%async_computation.3 | async-start | bytes 4194304 | tf_op jit(solution)/shard_map/psum | solution.py:16
  96.6 0.8 copy-start.6
  96.7 127.2 %reduce-scatter.2.cloned.1.call-start = ((), (), s32[]{:S(2)}) async-start(), calls=%async_computation.2 | async-start | bytes 5898240 | tf_op jit(solution)/shard_map/reduce_scatter | solution.py:59
  100.7 0.9 copy-start.7
  100.7 61.4 %copy-start = (bf16[128,4096]{1,0:T(8,128)(2,1)S(1)}, bf16[128,4096]{1,0:T(8,128)(2,1)}, u32[]{:S(2)}) copy-start(bf16[128,4096]{1,0:T(8,128)(2,1)} %all-gather.2.cloned.1.call-done) | copy-start | bytes 3145732
  162.1 1.8 copy-start.5
Sparse Core Ops, SparseCore 0:
  69.1 24.6 all-gather.1
  96.8 65.2 all-reduce.4
  164.4 59.4 reduce-scatter.1
where the time goes:
time: 233 us; the launch traced here: 232 us
  waiting for transfers between devices  144 us (62%)
  blocking collectives  56.3 us (24%)
  between operations  13.9 us (6%)
  other arithmetic  10.3 us (4%)
  matrix products  5.47 us (2%)
  local copies, waits for them, and re-layouts  2.51 us (1%)
    psum x1, waiting for transfers between devices, spread(): return lax.psum(kept, axis)  60.3 us
    reduce_scatter x1, waiting for transfers between devices, body(): lax.psum_scatter(lax.dot_general(genotype, expression, (((0,), (0,)), (()...  58.7 us
    psum x1, blocking collectives, body(): lax.psum((seen_now, summed_now, seen_prev, summed_prev, squares_trait), '...  30.3 us
    psum x1, blocking collectives, body(): lax.psum((jnp.sum(offset_now * offset_now, 0), jnp.sum(offset_prev * offs...  26 us
    all_gather x1, waiting for transfers between devices, body(): own_panel = lax.all_gather(scaled, 'col', axis=1, tiled=True)  24.8 us
  transfers between devices with their start and end apart: 3, of which 3 were waited for; matrix products, arithmetic and copies ran while one was open for 3% of the time, Pallas kernels for 0%

commit v1 on v0

v1 whole, which is shorter than its diff:
```python
import functools
import math

import jax
import jax.numpy as jnp
from jax import lax
from jax.experimental import pallas as pl
from jax.experimental.pallas import tpu as pltpu
from jax.sharding import PartitionSpec as P

epsilon = 1e-05
MESH = pl.DeviceIdType.MESH


def kernel(nrow, ncol, prior_ref, dn_ref, mn_ref, dp_ref, mp_ref, ex_ref, grm_ref, out_ref,
           stat, statp, panels, gt, inv, own, psend, precv, lsend, lrecv, gown, gsend, grecv,
           st_s, st_r, sp_s, sp_r, pr_s, pr_r, ln_s, ln_r, pan_s, pan_r, dup_s, dup_r, gr_s, gr_r):
    f32, bf16 = jnp.float32, jnp.bfloat16
    r, c = lax.axis_index("row"), lax.axis_index("col")
    z, k = r // 2, r % 2
    nz = nrow // 2
    partner = 2 * z + 1 - k
    rows, width = dn_ref.shape
    wide = dp_ref.shape[1]
    genes = ex_ref.shape[1]
    part = wide // nrow
    samples = rows * nrow

    def copy(src, dst, ssem, rsem, **where):
        return pltpu.make_async_remote_copy(
            src_ref=src, dst_ref=dst, send_sem=ssem, recv_sem=rsem,
            device_id=where, device_id_type=MESH)

    barrier = pltpu.get_barrier_semaphore()
    for o in range(1, nrow):
        pl.semaphore_signal(barrier, inc=1, device_id={"row": (r + o) % nrow}, device_id_type=MESH)
    for o in range(1, ncol):
        pl.semaphore_signal(barrier, inc=1, device_id={"col": (c + o) % ncol}, device_id_type=MESH)

    def local(d_ref, m_ref, at, size):
        v, w = d_ref[...].astype(f32), m_ref[...].astype(f32)
        n = jnp.sum(w, 0, keepdims=True)
        s = jnp.sum(w * v, 0, keepdims=True)
        off = w * (v - s / jnp.maximum(n, 1.0))
        stat[r, :, at:at + size] = n
        stat[r, :, at + size:at + 2 * size] = s
        stat[r, :, at + 2 * size:at + 3 * size] = jnp.sum(off * off, 0, keepdims=True)

    local(dp_ref, mp_ref, 0, wide)
    local(dn_ref, mn_ref, 3 * wide, width)
    pl.semaphore_wait(barrier, nrow + ncol - 2)

    def stat_copy(buf, ssem, rsem, slot, peer):
        return copy(buf.at[slot], buf.at[slot], ssem.at[peer], rsem.at[slot], row=peer)

    for o in range(1, nrow):
        stat_copy(stat, st_s, st_r, r, (r + o) % nrow).start()

    chunk = genes // 4
    for j in range(4):
        e = ex_ref[:, j * chunk:(j + 1) * chunk].astype(f32)
        statp[r, :, j * chunk:(j + 1) * chunk] = jnp.sum(e * e, 0, keepdims=True)
    for o in range(1, nrow):
        stat_copy(stat, st_s, st_r, (r + o) % nrow, (r + o) % nrow).wait_recv()

    def combine(at, size):
        n = [stat[q, :, at:at + size] for q in range(nrow)]
        s = [stat[q, :, at + size:at + 2 * size] for q in range(nrow)]
        observed = jnp.maximum(functools.reduce(jnp.add, n), 1.0)
        centre = functools.reduce(jnp.add, s) / observed
        second = jnp.zeros_like(centre)
        for q in range(nrow):
            gap = s[q] / jnp.maximum(n[q], 1.0) - centre
            second = second + (stat[q, :, at + 2 * size:at + 3 * size] + n[q] * gap * gap)
        return centre, lax.rsqrt(second / observed + epsilon)

    centre, scale = combine(0, wide)
    geno = mp_ref[...].astype(f32) * (dp_ref[...].astype(f32) - centre)
    geno = jnp.transpose(geno).astype(bf16)
    for d in range(nz):
        for q in range(2):
            gt[q, d * part:(d + 1) * part, :] = geno[(2 * d + q) * part:(2 * d + q + 1) * part, :]
    inv[...] = jnp.transpose(jnp.broadcast_to(scale, (rows, wide)))

    centre, scale = combine(3 * wide, width)
    panels[r] = (mn_ref[...].astype(f32) * (dn_ref[...].astype(f32) - centre) * scale).astype(bf16)

    def panel(slot, step):
        return copy(panels.at[slot], panels.at[slot], pan_s.at[slot], pan_r.at[slot],
                    row=r + 2 * step)

    def panel_back(slot):
        return copy(panels.at[slot], panels.at[slot], pan_s.at[nrow + slot], pan_r.at[slot],
                    row=r - 2)

    def dup(slot):
        return copy(panels.at[slot], panels.at[slot], dup_s.at[slot], dup_r.at[slot], row=partner)

    @pl.when(z < nz - 1)
    def _():
        panel(r, 1).start()

    @pl.when(z > 0)
    def _():
        panel_back(r).start()

    dup(r).start()

    other = gt[1 - k]
    for j in range(4):
        cols = slice(j * chunk, (j + 1) * chunk)
        psend[:, cols] = jnp.dot(other, ex_ref[:, cols], preferred_element_type=f32)

    def block(d):
        return pl.ds(pl.multiple_of(d * part, part), part)

    def pair(d):
        return copy(psend.at[block(d)], precv.at[block(d)], pr_s.at[d], pr_r.at[d], row=partner)

    order = [jnp.where(z < nz // 2, nz - 1 - i, i) for i in range(nz)]
    for i in range(nz):
        pair(order[i]).start()
    for o in range(1, nrow):
        stat_copy(statp, sp_s, sp_r, r, (r + o) % nrow).start()
    mine = gt[k]
    for j in range(4):
        cols = slice(j * chunk, (j + 1) * chunk)
        own[:, cols] = jnp.dot(mine, ex_ref[:, cols], preferred_element_type=f32)

    def line(d):
        target = jnp.where(d > z, z + 1, z - 1)
        slot = jnp.where(d == z - 1, nz, d)
        return copy(lsend.at[d], lrecv.at[slot], ln_s.at[d], ln_r.at[slot],
                    row=jnp.clip(2 * target + k, 0, nrow - 1))

    def line_wait(slot):
        copy(lsend.at[0], lrecv.at[slot], ln_s.at[0], ln_r.at[slot], row=partner).wait_recv()

    def cross_step(d):
        @pl.when(d != z)
        def _():
            pair(d).wait_recv()
            has = jnp.logical_or(jnp.logical_and(d > z, z > 0), jnp.logical_and(d < z, z < nz - 1))

            @pl.when(has)
            def _():
                line_wait(d)
                lsend[d] = (own[block(d), :] + precv[block(d), :] + lrecv[d].astype(f32)).astype(bf16)

            @pl.when(jnp.logical_not(has))
            def _():
                lsend[d] = (own[block(d), :] + precv[block(d), :]).astype(bf16)

            line(d).start()

    def gram(src, q):
        return copy(gsend.at[q], grecv.at[src], gr_s.at[q], gr_r.at[src], col=q)

    def gram_step(zz):
        dup(2 * zz + 1 - k).wait_recv()
        both = panels[pl.ds(2 * zz, 2)].reshape(2 * rows, width)
        value = lax.dot_general(panels[r], both, (((1,), (1,)), ((), ())), preferred_element_type=f32)

        @pl.when(zz == c)
        def _():
            gown[...] = value

        @pl.when(zz != c)
        def _():
            gsend[zz] = value
            gram(c, zz).start()

    def pan_wait(slot):
        copy(panels.at[slot], panels.at[slot], pan_s.at[slot], pan_r.at[slot], row=partner).wait_recv()

    cross_step(order[0])
    for t in range(1, nz):
        @pl.when(z - t >= 0)
        def _():
            slot = r - 2 * t
            pan_wait(slot)

            @pl.when(z < nz - 1)
            def _():
                panel(slot, 1).start()

            dup(slot).start()

        @pl.when(z + t < nz)
        def _():
            slot = r + 2 * t
            pan_wait(slot)

            @pl.when(z > 0)
            def _():
                panel_back(slot).start()

            dup(slot).start()

        if t == 1:
            gram_step(z)
        cross_step(order[t])

        @pl.when(z - t >= 0)
        def _():
            gram_step(z - t)

        @pl.when(z + t < nz)
        def _():
            gram_step(z + t)

    pair(z).wait_recv()
    power = statp[r]
    for o in range(1, nrow):
        q = (r + o) % nrow
        stat_copy(statp, sp_s, sp_r, q, q).wait_recv()
        power = power + statp[q]
    power = lax.rsqrt(power / samples + epsilon) / math.sqrt(samples)
    scale = inv[block(r), 0:1]

    @pl.when(z > 0)
    def _():
        line_wait(z)
        own[block(z), :] = own[block(z), :] + lrecv[z].astype(f32)

    @pl.when(z < nz - 1)
    def _():
        line_wait(nz)
        own[block(z), :] = own[block(z), :] + lrecv[nz].astype(f32)

    out_ref[...] = (own[block(z), :] + precv[block(z), :]) * scale * power

    total = gown[...]
    for o in range(1, ncol):
        src = (c + o) % ncol
        gram(src, src).wait_recv()
        total = total + grecv[src]
    grm_ref[...] = prior_ref[...] + total / (width * ncol)

    for o in range(1, nrow):
        q = (r + o) % nrow
        stat_copy(stat, st_s, st_r, r, q).wait_send()
        stat_copy(statp, sp_s, sp_r, r, q).wait_send()
    for d in range(nz):
        pair(d).wait_send()
        dup(2 * d + k).wait_send()

        @pl.when(d != z)
        def _():
            line(d).wait_send()

        @pl.when(jnp.logical_and(d <= z, z < nz - 1))
        def _():
            panel(2 * d + k, 1).wait_send()

        @pl.when(jnp.logical_and(d >= z, z > 0))
        def _():
            panel_back(2 * d + k).wait_send()
    for o in range(1, ncol):
        gram(c, (c + o) % ncol).wait_send()


def body(nrow, ncol, prior, dn, mn, dp, mp, ex):
    f32, bf16 = jnp.float32, jnp.bfloat16
    rows, width = dn.shape
    wide, genes = dp.shape[1], ex.shape[1]
    nz, part = nrow // 2, wide // nrow
    dma = pltpu.SemaphoreType.DMA
    scratch = [
        pltpu.VMEM((nrow, 1, 3 * (width + wide)), f32),
        pltpu.VMEM((nrow, 1, genes), f32),
        pltpu.VMEM((nrow, rows, width), bf16),
        pltpu.VMEM((2, nz * part, rows), bf16),
        pltpu.VMEM((wide, rows), f32),
        pltpu.VMEM((nz * part, genes), f32),
        pltpu.VMEM((nz * part, genes), f32),
        pltpu.VMEM((nz * part, genes), f32),
        pltpu.VMEM((nz, part, genes), bf16),
        pltpu.VMEM((nz + 1, part, genes), bf16),
        pltpu.VMEM(prior.shape, f32),
        pltpu.VMEM((ncol,) + prior.shape, f32),
        pltpu.VMEM((ncol,) + prior.shape, f32),
        dma((nrow,)), dma((nrow,)), dma((nrow,)), dma((nrow,)),
        dma((nz,)), dma((nz,)), dma((nz,)), dma((nz + 1,)),
        dma((2 * nrow,)), dma((nrow,)), dma((nrow,)), dma((nrow,)),
        dma((ncol,)), dma((ncol,)),
    ]
    vmem = pl.BlockSpec(memory_space=pltpu.VMEM)
    return pl.pallas_call(
        functools.partial(kernel, nrow, ncol),
        out_shape=(jax.ShapeDtypeStruct(prior.shape, f32), jax.ShapeDtypeStruct((part, genes), f32)),
        in_specs=[vmem] * 6,
        out_specs=(vmem, vmem),
        scratch_shapes=scratch,
        compiler_params=pltpu.CompilerParams(
            collective_id=0, has_side_effects=True, vmem_limit_bytes=66_000_000),
    )(prior, dn, mn, dp, mp, ex)


def solution(mesh):
    spec = P("row", "col")
    only = P("row", None)
    return jax.shard_map(
        functools.partial(body, mesh.shape["row"], mesh.shape["col"]),
        mesh=mesh, in_specs=(spec, spec, spec, only, only, spec), out_specs=(spec, spec),
        check_vma=False)
```

time: 233 us -> 64.7 us (0.28)
  waiting for transfers between devices: 144 us -> 0 us
  Pallas kernels: 0 us -> 59.4 us
  blocking collectives: 56.3 us -> 0 us
  between operations: 13.9 us -> 0.64 us
  other arithmetic: 10.3 us -> 0 us
  matrix products: 5.47 us -> 0 us
    psum x1 -> x0, waiting for transfers between devices: 60.3 us -> none  [spread(): return lax.psum(kept, axis)]
    pallas_call x0 -> x1, Pallas kernels: none -> 59.4 us  [body(): pl.pallas_call(functools.partial(kernel, nrow, ncol), out_shape=(jax.Shap...]
    reduce_scatter x1 -> x0, waiting for transfers between devices: 58.7 us -> none  [body(): lax.psum_scatter(lax.dot_general(genotype, expression, (((0,), (0,)), (()...]
    psum x2 -> x0, blocking collectives: 56.3 us -> none  [the longest x1 30.3 us: body(): lax.psum((seen_now, summed_now, seen_prev, summed_prev, squares_trait), '...]
    all_gather x1 -> x0, waiting for transfers between devices: 24.8 us -> none  [body(): own_panel = lax.all_gather(scaled, 'col', axis=1, tiled=True)]
    dot_general x3 -> x0, matrix products: 5.47 us -> none  [the longest x1 3.18 us: body(): lax.dot_general(genotype, expression, (((0,), (0,)), ((), ())), preferred...]
    reduce_sum x5 -> x0, other arithmetic: 4.59 us -> none  [the longest x2 2.33 us: local_sums(): return (values, weight, jnp.sum(weight, 0), jnp.sum(weight * values, 0))]
    select_n x1 -> x0, other arithmetic: 2.76 us -> none  [spread(): jnp.where(lax.axis_index(axis) == source, value, 0).astype(value.dtype)]
  transfers between devices with their start and end apart: 3 -> 0, of which waited for: 3 -> 0; matrix products, arithmetic and copies ran while one was open for 3% -> 0% of each run, Pallas kernels for 0% -> 0%
where the time goes in v1:
time: 64.7 us; the launch traced here: 63.6 us
  Pallas kernels  59.4 us (92%)
  local copies, waits for them, and re-layouts  3.53 us (5%)
    pallas_call x1, Pallas kernels, body(): pl.pallas_call(functools.partial(kernel, nrow, ncol), out_shape=(jax.Shap...  59.4 us
    unnamed x2, local copies, waits for them, and re-layouts  3.53 us

profile of v1, /device:TPU:0, one launch (start us, length us, event | category | flops | bytes accessed | tf_op | source)
XLA Modules:
  0.0 63.6 jit_solution(6552387365726695300)
XLA Ops:
  0.6 59.4 %shard_map.77 = (f32[128,256]{1,0:T(8,128)}, f32[32,5120]{1,0:T(8,128)}) custom-call(f32[128,256]{1,0:T(8,128)} %prior_ref.1, bf16[128,1024]{1,0:T(8,128)(2,1)} %dn_ref.1, s32[128,1024]{1,0:T(8,128)} %mn_ref.1, bf16[128,256]{1,0:T(8,128)(2,1)} %dp_ref.1, s32[128,256]{1,0:T(8,128)} %mp_ref.1, bf16[128,5120]{1,0:T(8,128)(2,1)} %ex_ref.1), custom_call_target="tpu_custom_call" | custom-call | tf_op jit(solution)/shard_map/pallas_call | solution.py:289
  60.1 1.6 %copy.10 = f32[128,256]{1,0:T(8,128)} copy(f32[128,256]{1,0:T(8,128)} %get-tuple-element.4) | data formatting | bytes 262144
  61.6 2.0 %copy.11 = f32[32,5120]{1,0:T(8,128)} copy(f32[32,5120]{1,0:T(8,128)} %get-tuple-element.5) | data formatting | bytes 1310720

commit v2 on v1

v2 whole, which is shorter than its diff:
```python
import functools
import math

import jax
import jax.numpy as jnp
from jax import lax
from jax.experimental import pallas as pl
from jax.experimental.pallas import tpu as pltpu
from jax.sharding import PartitionSpec as P

epsilon = 1e-05
MESH = pl.DeviceIdType.MESH


HALVES = 2


def kernel(nrow, ncol, dn_hbm, mn_hbm, dp_hbm, mp_hbm, ex_hbm, gram_ref, out_ref,
           dn_ref, mn_ref, dp_ref, mp_ref, ex_ref,
           statq, stat, pw, pws, pwr, panels, gt, inv, own, psend, precv, lsend, lrecv,
           gsend, grecv, in_s,
           sq_s, sq_r, st_s, st_r, pw_s, pw_r, pr_s, pr_r, ln_s, ln_r, pan_s, pan_r, dup_s, dup_r,
           gr_s, gr_r):
    f32, bf16 = jnp.float32, jnp.bfloat16
    r, c = lax.axis_index("row"), lax.axis_index("col")
    z, k = r // 2, r % 2
    nz = nrow // 2
    partner = 2 * z + 1 - k
    rows, width = dn_ref.shape
    wide = dp_ref.shape[1]
    genes = ex_ref.shape[1]
    part = wide // nrow
    half = genes // HALVES
    samples = rows * nrow
    first, last = z == 0, z == nz - 1
    inner = jnp.logical_and(z > 0, z < nz - 1)

    def copy(src, dst, ssem, rsem, **where):
        return pltpu.make_async_remote_copy(
            src_ref=src, dst_ref=dst, send_sem=ssem, recv_sem=rsem,
            device_id=where, device_id_type=MESH)

    barrier = pltpu.get_barrier_semaphore()
    for o in range(1, nrow):
        pl.semaphore_signal(barrier, inc=1, device_id={"row": (r + o) % nrow}, device_id_type=MESH)
    for o in range(1, ncol):
        pl.semaphore_signal(barrier, inc=1, device_id={"col": (c + o) % ncol}, device_id_type=MESH)
    fetch = [pltpu.make_async_copy(a, b, in_s.at[i]) for i, (a, b) in enumerate((
        (dp_hbm, dp_ref), (mp_hbm, mp_ref), (dn_hbm, dn_ref), (mn_hbm, mn_ref), (ex_hbm, ex_ref)))]
    for f in fetch:
        f.start()

    def local(d_ref, m_ref, buf, size):
        v, w = d_ref[...].astype(f32), m_ref[...].astype(f32)
        n = jnp.sum(w, 0, keepdims=True)
        s = jnp.sum(w * v, 0, keepdims=True)
        off = w * (v - s / jnp.maximum(n, 1.0))
        buf[r, :, 0:size] = n
        buf[r, :, size:2 * size] = s
        buf[r, :, 2 * size:3 * size] = jnp.sum(off * off, 0, keepdims=True)

    def stat_copy(buf, ssem, rsem, slot, peer):
        return copy(buf.at[slot], buf.at[slot], ssem.at[peer], rsem.at[slot], row=peer)

    def send_stats(buf, ssem, rsem):
        for o in range(1, nrow):
            stat_copy(buf, ssem, rsem, r, (r + o) % nrow).start()

    def wait_stats(buf, ssem, rsem):
        for o in range(1, nrow):
            q = (r + o) % nrow
            stat_copy(buf, ssem, rsem, q, q).wait_recv()

    fetch[0].wait()
    fetch[1].wait()
    local(dp_ref, mp_ref, statq, wide)
    pl.semaphore_wait(barrier, nrow + ncol - 2)
    send_stats(statq, sq_s, sq_r)
    fetch[2].wait()
    fetch[3].wait()
    local(dn_ref, mn_ref, stat, width)
    send_stats(stat, st_s, st_r)
    fetch[4].wait()
    chunk = genes // 4
    for j in range(4):
        e = ex_ref[:, j * chunk:(j + 1) * chunk].astype(f32)
        pw[0, :, j * chunk:(j + 1) * chunk] = jnp.sum(e * e, 0, keepdims=True)
    pw_pair = copy(pw.at[0], pw.at[1], pw_s.at[0], pw_r.at[0], row=partner)
    pw_pair.start()

    def combine(buf, size):
        n = [buf[q, :, 0:size] for q in range(nrow)]
        s = [buf[q, :, size:2 * size] for q in range(nrow)]
        observed = jnp.maximum(functools.reduce(jnp.add, n), 1.0)
        centre = functools.reduce(jnp.add, s) / observed
        second = jnp.zeros_like(centre)
        for q in range(nrow):
            gap = s[q] / jnp.maximum(n[q], 1.0) - centre
            second = second + (buf[q, :, 2 * size:3 * size] + n[q] * gap * gap)
        return centre, lax.rsqrt(second / observed + epsilon)

    wait_stats(statq, sq_s, sq_r)
    centre, scale = combine(statq, wide)
    geno = mp_ref[...].astype(f32) * (dp_ref[...].astype(f32) - centre)
    geno = jnp.transpose(geno).astype(bf16)
    for d in range(nz):
        for q in range(2):
            gt[q, d * part:(d + 1) * part, :] = geno[(2 * d + q) * part:(2 * d + q + 1) * part, :]

    def pair(d, h):
        return copy(psend.at[d, h], precv.at[d, h], pr_s.at[d, h], pr_r.at[d, h], row=partner)

    def products(lhs, dst, h):
        cols = slice(h * half, (h + 1) * half)
        value = jnp.dot(lhs, ex_ref[:, cols], preferred_element_type=f32)
        for d in range(nz):
            dst[d, h] = value[d * part:(d + 1) * part, :]

    other = gt[1 - k]
    outward = sorted(range(nz), key=lambda d: min(d, nz - 1 - d))
    for h in range(HALVES):
        products(other, psend, h)
        for d in outward:
            pair(d, h).start()

    def panel(slot):
        return copy(panels.at[slot], panels.at[slot], pan_s.at[slot], pan_r.at[slot], row=r + 2)

    def panel_back(slot):
        return copy(panels.at[slot], panels.at[slot], pan_s.at[nrow + slot], pan_r.at[slot],
                    row=r - 2)

    def dup(slot):
        return copy(panels.at[slot], panels.at[slot], dup_s.at[slot], dup_r.at[slot], row=partner)

    def pan_wait(slot):
        copy(panels.at[slot], panels.at[slot], pan_s.at[slot], pan_r.at[slot], row=partner).wait_recv()

    wait_stats(stat, st_s, st_r)
    centre, scale_now = combine(stat, width)
    panels[r] = (mn_ref[...].astype(f32) * (dn_ref[...].astype(f32) - centre) * scale_now).astype(bf16)

    @pl.when(jnp.logical_not(last))
    def _():
        panel(r).start()

    @pl.when(jnp.logical_not(first))
    def _():
        panel_back(r).start()

    dup(r).start()
    mine = gt[k]
    for h in range(HALVES):
        products(mine, own, h)
    inv[...] = jnp.transpose(jnp.broadcast_to(scale, (rows, wide)))

    pw_pair.wait()
    pw[0] = pw[0] + pw[1]

    def pw_line(way):
        return copy(pws.at[way], pwr.at[way], pw_s.at[1 + way], pw_r.at[1 + way],
                    row=jnp.clip(r + 2 - 4 * way, 0, nrow - 1))

    def line(d, h, way):
        if way == 0:
            slot = d
        else:
            slot = jnp.where(d == z - 1, nz, d)
        return copy(lsend.at[d, h], lrecv.at[slot, h], ln_s.at[d, h], ln_r.at[slot, h],
                    row=jnp.clip(r + 2 - 4 * way, 0, nrow - 1))

    def line_wait(slot, h):
        copy(lsend.at[0, h], lrecv.at[slot, h], ln_s.at[0, h], ln_r.at[slot, h], row=partner).wait_recv()

    def start_line(d, h, way):
        pair(d, h).wait_recv()
        lsend[d, h] = (own[d, h] + precv[d, h]).astype(bf16)
        line(d, h, way).start()

    def pass_line(d, h, way):
        pair(d, h).wait_recv()
        value = own[d, h] + precv[d, h]
        line_wait(d, h)
        lsend[d, h] = (value + lrecv[d, h].astype(f32)).astype(bf16)
        line(d, h, way).start()

    for way, end in ((0, first), (1, last)):
        @pl.when(end)
        def _():
            pws[way] = pw[0]
            pw_line(way).start()
            for h in range(HALVES):
                for d in (range(nz - 1, 0, -1) if way == 0 else range(nz - 1)):
                    start_line(d, h, way)

    def gram(src, q):
        return copy(gsend.at[q], grecv.at[src], gr_s.at[q], gr_r.at[src], col=q)

    def gram_step(zz):
        dup(2 * zz + 1 - k).wait_recv()
        both = panels[pl.ds(2 * zz, 2)].reshape(2 * rows, width)
        value = lax.dot_general(panels[r], both, (((1,), (1,)), ((), ())), preferred_element_type=f32)

        @pl.when(zz == c)
        def _():
            gram_ref[...] = value

        @pl.when(zz != c)
        def _():
            gsend[zz] = value
            gram(c, zz).start()

    def hop(t):
        @pl.when(z - t >= 0)
        def _():
            slot = r - 2 * t
            pan_wait(slot)

            @pl.when(jnp.logical_not(last))
            def _():
                panel(slot).start()

            dup(slot).start()

        @pl.when(z + t < nz)
        def _():
            slot = r + 2 * t
            pan_wait(slot)

            @pl.when(jnp.logical_not(first))
            def _():
                panel_back(slot).start()

            dup(slot).start()

    def near(t):
        if t == 0:
            gram_step(z)
            return

        @pl.when(z - t >= 0)
        def _():
            gram_step(z - t)

        @pl.when(z + t < nz)
        def _():
            gram_step(z + t)

    low = jnp.logical_and(inner, z < nz // 2)
    high = jnp.logical_and(inner, z >= nz // 2)

    def pass_pw(way):
        copy(pws.at[way], pwr.at[way], pw_s.at[1 + way], pw_r.at[1 + way], row=partner).wait_recv()
        pws[way] = pw[0] + pwr[way]
        pw_line(way).start()

    def pass_key(m, way, when):
        if m == 0:
            @pl.when(when)
            def _():
                pass_pw(way)

        @pl.when(jnp.logical_and(when, (z < nz - 1 - m) if way == 0 else (z > m)))
        def _():
            for h in range(HALVES):
                pass_line(nz - 1 - m if way == 0 else m, h, way)

    for m in range(nz - 1):
        hop(m + 1)
        pass_key(m, 0, low)
        pass_key(m, 1, high)
        near(m)
    for m in range(nz - 1):
        pass_key(m, 1, low)
        pass_key(m, 0, high)
    near(nz - 1)

    total = gram_ref[...]
    for o in range(1, ncol):
        src = (c + o) % ncol
        gram(src, src).wait_recv()
        total = total + grecv[src]
    gram_ref[...] = total

    def pw_wait(way):
        copy(pws.at[way], pwr.at[way], pw_s.at[1 + way], pw_r.at[1 + way], row=partner).wait_recv()
        pw[0] = pw[0] + pwr[way]

    @pl.when(first)
    def _():
        pw_wait(1)

    @pl.when(last)
    def _():
        pw_wait(0)

    @pl.when(inner)
    def _():
        pw[0] = pw[0] + pwr[0] + pwr[1]

    power = lax.rsqrt(pw[0] / samples + epsilon) / math.sqrt(samples)
    scale = inv[pl.ds(pl.multiple_of(r * part, part), part), 0:1]
    for h in range(HALVES):
        pair(z, h).wait_recv()

        @pl.when(z > 0)
        def _():
            line_wait(z, h)
            own[z, h] = own[z, h] + lrecv[z, h].astype(f32)

        @pl.when(z < nz - 1)
        def _():
            line_wait(nz, h)
            own[z, h] = own[z, h] + lrecv[nz, h].astype(f32)

        out_ref[:, h * half:(h + 1) * half] = (
            (own[z, h] + precv[z, h]) * scale * power[:, h * half:(h + 1) * half])


    @pl.when(jnp.logical_not(last))
    def _():
        pw_line(0).wait_send()

    @pl.when(jnp.logical_not(first))
    def _():
        pw_line(1).wait_send()

    for o in range(1, nrow):
        q = (r + o) % nrow
        stat_copy(statq, sq_s, sq_r, r, q).wait_send()
        stat_copy(stat, st_s, st_r, r, q).wait_send()
    for d in range(nz):
        dup(2 * d + k).wait_send()
        for h in range(HALVES):
            pair(d, h).wait_send()

            @pl.when(d > z)
            def _():
                line(d, h, 0).wait_send()

            @pl.when(d < z)
            def _():
                line(d, h, 1).wait_send()

        @pl.when(jnp.logical_and(d <= z, z < nz - 1))
        def _():
            panel(2 * d + k).wait_send()

        @pl.when(jnp.logical_and(d >= z, z > 0))
        def _():
            panel_back(2 * d + k).wait_send()
    for o in range(1, ncol):
        gram(c, (c + o) % ncol).wait_send()


def finish(variants, prior_hbm, gram_hbm, cross_hbm, grm_ref, out_ref, prior_ref, gram_ref, in_s):
    fetch = [pltpu.make_async_copy(a, b, in_s.at[i]) for i, (a, b) in enumerate((
        (cross_hbm, out_ref), (prior_hbm, prior_ref), (gram_hbm, gram_ref)))]
    for f in fetch:
        f.start()
    fetch[1].wait()
    fetch[2].wait()
    grm_ref[...] = prior_ref[...] + gram_ref[...] / variants
    fetch[0].wait()


def body(nrow, ncol, prior, dn, mn, dp, mp, ex):
    f32, bf16 = jnp.float32, jnp.bfloat16
    rows, width = dn.shape
    wide, genes = dp.shape[1], ex.shape[1]
    nz, part, half = nrow // 2, wide // nrow, genes // HALVES
    dma = pltpu.SemaphoreType.DMA
    scratch = [pltpu.VMEM(a.shape, a.dtype) for a in (dn, mn, dp, mp, ex)] + [
        pltpu.VMEM((nrow, 1, 3 * wide), f32),
        pltpu.VMEM((nrow, 1, 3 * width), f32),
        pltpu.VMEM((2, 1, genes), f32),
        pltpu.VMEM((2, 1, genes), f32),
        pltpu.VMEM((2, 1, genes), f32),
        pltpu.VMEM((nrow, rows, width), bf16),
        pltpu.VMEM((2, nz * part, rows), bf16),
        pltpu.VMEM((wide, rows), f32),
        pltpu.VMEM((nz, HALVES, part, half), f32),
        pltpu.VMEM((nz, HALVES, part, half), f32),
        pltpu.VMEM((nz, HALVES, part, half), f32),
        pltpu.VMEM((nz, HALVES, part, half), bf16),
        pltpu.VMEM((nz + 1, HALVES, part, half), bf16),
        pltpu.VMEM((ncol,) + prior.shape, f32),
        pltpu.VMEM((ncol,) + prior.shape, f32),
        dma((5,)),
        dma((nrow,)), dma((nrow,)), dma((nrow,)), dma((nrow,)), dma((3,)), dma((3,)),
        dma((nz, HALVES)), dma((nz, HALVES)), dma((nz, HALVES)), dma((nz + 1, HALVES)),
        dma((2 * nrow,)), dma((nrow,)), dma((nrow,)), dma((nrow,)),
        dma((ncol,)), dma((ncol,)),
    ]
    vmem = pl.BlockSpec(memory_space=pltpu.VMEM)
    hbm = pl.BlockSpec(memory_space=pltpu.HBM)
    gram, cross = pl.pallas_call(
        functools.partial(kernel, nrow, ncol),
        out_shape=(jax.ShapeDtypeStruct(prior.shape, f32), jax.ShapeDtypeStruct((part, genes), f32)),
        in_specs=[hbm] * 5,
        out_specs=(vmem,) * 2,
        scratch_shapes=scratch,
        compiler_params=pltpu.CompilerParams(
            collective_id=0, has_side_effects=True, vmem_limit_bytes=66000000),
    )(dn, mn, dp, mp, ex)
    return pl.pallas_call(
        functools.partial(finish, width * ncol),
        out_shape=(jax.ShapeDtypeStruct(prior.shape, f32), jax.ShapeDtypeStruct((part, genes), f32)),
        in_specs=[hbm] * 3,
        out_specs=(vmem,) * 2,
        scratch_shapes=[pltpu.VMEM(prior.shape, f32), pltpu.VMEM(prior.shape, f32), dma((3,))],
        compiler_params=pltpu.CompilerParams(vmem_limit_bytes=66000000),
    )(prior, gram, cross)


def solution(mesh):
    spec = P("row", "col")
    only = P("row", None)
    return jax.shard_map(
        functools.partial(body, mesh.shape["row"], mesh.shape["col"]),
        mesh=mesh, in_specs=(spec, spec, spec, only, only, spec), out_specs=(spec, spec),
        check_vma=False)
```

time: 64.7 us -> 52.3 us (0.81); the launches traced: 63.6 us -> 51.9 us
  Pallas kernels: 59.4 us -> 51.3 us
  local copies, waits for them, and re-layouts: 3.53 us -> 0 us
    pallas_call x1, Pallas kernels: 59.4 us -> 49.2 us  [body(): pl.pallas_call(functools.partial(kernel, nrow, ncol), out_shape=(jax.Shap...]
    unnamed x2 -> x0, local copies, waits for them, and re-layouts: 3.53 us -> none
    pallas_call x0 -> x1, Pallas kernels: none -> 2.06 us  [body(): pl.pallas_call(functools.partial(finish, width * ncol), out_shape=(jax.Sh...]
where the time goes in v2:
time: 52.3 us; the launch traced here: 51.9 us
  Pallas kernels  51.3 us (98%)
  between operations  0.64 us (1%)
    pallas_call x1, Pallas kernels, body(): pl.pallas_call(functools.partial(kernel, nrow, ncol), out_shape=(jax.Shap...  49.2 us
    pallas_call x1, Pallas kernels, body(): pl.pallas_call(functools.partial(finish, width * ncol), out_shape=(jax.Sh...  2.06 us

profile of v2, /device:TPU:0, one launch (start us, length us, event | category | flops | bytes accessed | tf_op | source)
XLA Modules:
  0.0 51.9 jit_solution(4471740595125139355)
XLA Ops:
  0.6 49.2 %shard_map.77 = (f32[128,256]{1,0:T(8,128)}, f32[32,5120]{1,0:T(8,128)}) custom-call(bf16[128,1024]{1,0:T(8,128)(2,1)} %dn_hbm.1, s32[128,1024]{1,0:T(8,128)} %mn_hbm.1, bf16[128,256]{1,0:T(8,128)(2,1)} %dp_hbm.1, s32[128,256]{1,0:T(8,128)} %mp_hbm.1, bf16[128,5120]{1,0:T(8,128)(2,1)} %ex_hbm.1), custom_call_target="tpu_custom_call" | custom-call | tf_op jit(solution)/shard_map/pallas_call | solution.py:397
  49.9 2.1 %shard_map.78 = (f32[128,256]{1,0:T(8,128)}, f32[32,5120]{1,0:T(8,128)}) custom-call(f32[128,256]{1,0:T(8,128)} %prior_hbm.1, f32[128,256]{1,0:T(8,128)} %get-tuple-element.4.gram_hbm, f32[32,5120]{1,0:T(8,128)} %get-tuple-element.5.cross_hbm), custom_call_target="tpu_custom_call" | custom-call | tf_op jit(solution)/shard_map/pallas_call | solution.py:406
